TPU v7x, 32 devices: a whole 2x2x4 slice. The times are simulated.
32 devices in a mesh: cut: 8 (over z, y), sub: 4 (over x, core).
Axes of the slice: x: 2, y: 2, z: 4, core: 2. Of those that a mesh axis runs over, the one named last changes fastest.
Arguments:
- residual: bfloat16 [8, 4, 1024, 128], P('cut', 'sub'), may hold values from -6 to 6
- inner_inverse: bfloat16 [8, 4, 4, 343, 343], P('cut', 'sub'), may hold values from -0.3125 to 0.3125
- inner_index: int32 [8, 4, 4, 343], P('cut', 'sub'), may hold values from 0 to 1023
- slab_dofs: int32 [8, 4, 5, 512], P('cut', 'sub'), may hold values from 0 to 1023
- face_inverse: bfloat16 [8, 4, 5, 3, 343, 343], P('cut', 'sub'), may hold values from -0.3125 to 0.3125
- face_index: int32 [8, 4, 5, 3, 343], P('cut', 'sub'), may hold values from 0 to 1023
- face_count: int32 [8, 4, 5], P('cut', 'sub'), may hold values from 1 to 3
Outputs:
- correction: float32 [8, 4, 1024, 128], P('cut', 'sub')
All inputs are finite; a program needn't handle non-finite values.
Results may differ from a plain program's by a relative error of at most 0.0003.
Values may be sent and summed in bfloat16 or wider, within the bound.
A program may use at most 64 MiB of HBM per device.

v0:
```python
import jax
import jax.numpy as jnp
from jax import lax
from jax.experimental import pallas as pl
from jax.experimental.pallas import tpu as pltpu
from jax.sharding import PartitionSpec as P

CUTLV = 3
LANES = 128
CHUNK = 128
INDEX = jnp.int16
STEPS = 32766.0
FLOOR = 1e-30
MESH = pl.DeviceIdType.MESH


def round_up(value, step):
    return (value + step - 1) // step * step


def split_pair(values):
    high = values.astype(jnp.bfloat16)
    low = (values - high.astype(jnp.float32)).astype(jnp.bfloat16)
    return high, low


def make_kernel(ndof, nrhs, nint, star, levels, slots, slab, early, order, finish):
    pad = round_up(star, LANES)
    joint = 2 * slab

    def kernel(
        res, inner_inv, inner_idx, dofs, face_inv, face_idx, counts, out,
        inv_in, inv_face, rows, res_t, st_in, st_face, p_t,
        gathered, pair, joined, kept, terms, peaks, back, back_peaks, acc,
        inv_sem, send_sem, recv_sem, give_sem, back_sem, peak_sem, back_peak_sem,
    ):
        copies = [pltpu.make_async_copy(inner_inv.at[0, 0], inv_in, inv_sem.at[levels])]
        for k in range(levels):
            copies.append(
                pltpu.make_async_copy(face_inv.at[0, 0, k], inv_face.at[k], inv_sem.at[k])
            )
        for copy in copies:
            copy.start()

        places = []
        for k in range(levels):
            axis = "cut" if k < CUTLV else "sub"
            bits = lax.axis_size(axis).bit_length() - 1
            apart = bits - 1 - (k if k < CUTLV else k - CUTLV)
            me = lax.axis_index(axis)
            upper = lax.rem(lax.div(me, 1 << apart), 2)
            far = me + (1 - 2 * upper) * (1 << apart)
            places.append(({axis: far}, upper, 1 - upper))

        barrier = pltpu.get_barrier_semaphore()
        for target, _, _ in places:
            pl.semaphore_signal(barrier, inc=1, device_id=target, device_id_type=MESH)

        def down(row, first, height):
            shape = (height, row.shape[1])
            spots = (lax.broadcasted_iota(jnp.int32, shape, 0) + first).astype(INDEX)
            wanted = jnp.broadcast_to(row, shape).astype(INDEX)
            one, zero = jnp.bfloat16(1), jnp.bfloat16(0)
            return jnp.where(wanted == spots, one, zero)

        def build_slab(k):
            def step(i, carry):
                first = pl.multiple_of(i * CHUNK, CHUNK)
                p_t[k, pl.ds(first, CHUNK), :] = down(dofs[k], first, CHUNK)
                return carry

            lax.fori_loop(0, ndof // CHUNK, step, 0)

        def build_stars(target, row_of, count, height):
            def step(i, carry):
                first = pl.multiple_of(i * CHUNK, CHUNK)
                for j in range(count):
                    row = rows[row_of + j : row_of + j + 1, :]
                    target[pl.ds(first, CHUNK), j * pad : (j + 1) * pad] = down(row, first, CHUNK)
                return carry

            lax.fori_loop(0, height // CHUNK, step, 0)

        def build_face(k):
            build_stars(st_face.at[k], nint + k * slots, slots, joint)

        send, give, give_peak = [], [], []
        for k, (target, own, far) in enumerate(places):
            send.append(
                pltpu.make_async_remote_copy(
                    src_ref=joined.at[k, own],
                    dst_ref=joined.at[k, own],
                    send_sem=send_sem.at[k],
                    recv_sem=recv_sem.at[k],
                    device_id=target,
                    device_id_type=MESH,
                )
            )
            give.append(
                pltpu.make_async_remote_copy(
                    src_ref=terms.at[k],
                    dst_ref=back.at[k],
                    send_sem=give_sem.at[k],
                    recv_sem=back_sem.at[k],
                    device_id=target,
                    device_id_type=MESH,
                )
            )

            give_peak.append(
                pltpu.make_async_remote_copy(
                    src_ref=peaks.at[k],
                    dst_ref=back_peaks.at[k],
                    send_sem=peak_sem.at[k],
                    recv_sem=back_peak_sem.at[k],
                    device_id=target,
                    device_id_type=MESH,
                )
            )

        res_t[...] = res[0, 0].T
        for k, (_, own, _) in enumerate(places):
            build_slab(k)
            if k == 1:
                pl.semaphore_wait(barrier, levels)
            if k >= 1:
                send[k - 1].start()
            mine = jnp.dot(res_t[...], p_t[k], preferred_element_type=jnp.float32)
            joined[k, own] = mine.astype(jnp.bfloat16)

        rows[...] = jnp.full(rows.shape, -1, jnp.int32)
        rows[0:nint, 0:star] = inner_idx[0, 0]
        for k in range(levels):
            for j in range(slots):
                at = nint + k * slots + j
                live = j < counts[0, 0, k]
                rows[at : at + 1, 0:star] = jnp.where(live, face_idx[k * slots + j], -1)
        pair[...] = jnp.zeros(pair.shape, jnp.bfloat16)
        send[levels - 1].start()

        def solve(picked, inverses, count):
            gathered[:, 0 : count * pad] = picked.astype(jnp.bfloat16)
            for j in range(count):
                solved = lax.dot_general(
                    inverses[j],
                    gathered[:, j * pad : j * pad + star],
                    (((1,), (1,)), ((), ())),
                    preferred_element_type=jnp.float32,
                )
                high, low = split_pair(solved)
                pair[j * pad : j * pad + star, 0:nrhs] = high
                pair[j * pad : j * pad + star, nrhs : 2 * nrhs] = low

        def face(k):
            _, own, far = places[k]
            send[k].wait_recv()
            copies[1 + k].wait()
            picked = jnp.dot(
                joined[k, 0], st_face[k, 0:slab, :], preferred_element_type=jnp.float32
            ) + jnp.dot(
                joined[k, 1], st_face[k, slab:joint, :], preferred_element_type=jnp.float32
            )
            solve(picked, inv_face.at[k], slots)
            def half_terms(half):
                at = pl.multiple_of(half * slab, slab)
                both = jnp.dot(
                    st_face[k, pl.ds(at, slab), :],
                    pair[0 : slots * pad],
                    preferred_element_type=jnp.float32,
                )
                return both[:, :nrhs] + both[:, nrhs:]

            given = half_terms(far)
            peak = jnp.maximum(jnp.max(jnp.abs(given), axis=0, keepdims=True), FLOOR)
            peaks[k] = jnp.broadcast_to(peak, peaks.shape[1:])
            terms[k] = jnp.round(given * (STEPS / peak)).astype(jnp.int32).astype(jnp.int16)
            kept[k] = half_terms(own)
            give_peak[k].start()
            give[k].start()

        for k in early:
            build_face(k)
        build_stars(st_in, 0, nint, ndof)
        copies[0].wait()
        solve(
            jnp.dot(res_t[...], st_in[...], preferred_element_type=jnp.float32), inv_in, nint
        )
        acc[...] = jnp.dot(
            st_in[...], pair[0 : nint * pad], preferred_element_type=jnp.float32
        )
        for k in order:
            if k not in early:
                build_face(k)
            face(k)

        for k in finish:
            give_peak[k].wait_recv()
            give[k].wait_recv()
            unit = back_peaks[k, 0:1, :] * (1.0 / STEPS)
            returned = back[k].astype(jnp.int32).astype(jnp.float32) * unit
            high, low = split_pair(kept[k] + returned)
            pair[0:slab, 0:nrhs] = high
            pair[0:slab, nrhs : 2 * nrhs] = low
            both = jnp.dot(p_t[k], pair[0:slab], preferred_element_type=jnp.float32)
            if k == finish[-1]:
                both = acc[...] + both
                out[0, 0] = both[:, :nrhs] + both[:, nrhs:]
            else:
                acc[...] += both
        for k in range(levels):
            send[k].wait_send()
            give[k].wait_send()
            give_peak[k].wait_send()

    return kernel


def on_device(
    residual, inner_inverse, inner_index, slab_dofs, face_inverse, face_index, face_count
):
    ndof, nrhs = residual.shape[2:]
    nint, star = inner_index.shape[2:]
    levels, slots = face_index.shape[2:4]
    slab = slab_dofs.shape[3]
    pad = round_up(star, LANES)
    joint = 2 * slab
    index_rows = round_up(nint + levels * slots, 8)
    early, order, finish = (0, 1), (4, 3, 0, 1, 2), (4, 3, 0, 1, 2)
    kinds = jnp.bfloat16
    vmem = pl.BlockSpec(memory_space=pltpu.VMEM)
    anywhere = pl.BlockSpec(memory_space=pl.ANY)
    scalar = pl.BlockSpec(memory_space=pltpu.SMEM)
    most = max(nint, slots) * pad
    return pl.pallas_call(
        make_kernel(ndof, nrhs, nint, star, levels, slots, slab, early, order, finish),
        out_shape=jax.ShapeDtypeStruct(residual.shape, jnp.float32),
        in_specs=[vmem, anywhere, vmem, vmem, anywhere, vmem, scalar],
        out_specs=vmem,
        scratch_shapes=[
            pltpu.VMEM((nint, star, star), kinds),
            pltpu.VMEM((levels, slots, star, star), kinds),
            pltpu.VMEM((index_rows, pad), jnp.int32),
            pltpu.VMEM((nrhs, ndof), kinds),
            pltpu.VMEM((ndof, nint * pad), kinds),
            pltpu.VMEM((levels, joint, slots * pad), kinds),
            pltpu.VMEM((levels, ndof, slab), kinds),
            pltpu.VMEM((nrhs, most), kinds),
            pltpu.VMEM((max(most, slab), 2 * nrhs), kinds),
            pltpu.VMEM((levels, 2, nrhs, slab), kinds),
            pltpu.VMEM((levels, slab, nrhs), jnp.float32),
            pltpu.VMEM((levels, slab, nrhs), jnp.int16),
            pltpu.VMEM((levels, 8, nrhs), jnp.float32),
            pltpu.VMEM((levels, slab, nrhs), jnp.int16),
            pltpu.VMEM((levels, 8, nrhs), jnp.float32),
            pltpu.VMEM((ndof, 2 * nrhs), jnp.float32),
            pltpu.SemaphoreType.DMA((levels + 1,)),
            pltpu.SemaphoreType.DMA((levels,)),
            pltpu.SemaphoreType.DMA((levels,)),
            pltpu.SemaphoreType.DMA((levels,)),
            pltpu.SemaphoreType.DMA((levels,)),
            pltpu.SemaphoreType.DMA((levels,)),
            pltpu.SemaphoreType.DMA((levels,)),
        ],
        compiler_params=pltpu.CompilerParams(
            collective_id=0, has_side_effects=True, vmem_limit_bytes=64000000
        ),
    )(
        residual,
        inner_inverse,
        inner_index,
        slab_dofs.reshape(levels, 1, slab),
        face_inverse,
        face_index.reshape(levels * slots, 1, star),
        face_count,
    )


def solution(mesh):
    return jax.shard_map(
        on_device,
        mesh=mesh,
        in_specs=(
            P("cut", "sub", None, None),
            P("cut", "sub", None, None, None),
            P("cut", "sub", None, None),
            P("cut", "sub", None, None),
            P("cut", "sub", None, None, None, None),
            P("cut", "sub", None, None, None),
            P("cut", "sub", None),
        ),
        out_specs=P("cut", "sub", None, None),
        check_vma=False,
    )
```

profile of v0, /device:TPU:0, one launch (start us, length us, event | category | flops | bytes accessed | tf_op | source)
XLA Modules:
  0.0 30.8 jit_solution(6608332295991750886)
XLA Ops:
  0.0 2.4 %copy.8.inner_inv = bf16[1,1,4,343,343]{4,3,2,1,0:T(8,128)(2,1)} copy(bf16[1,1,4,343,343]{4,2,3,1,0:T(4,128)(2,1)} %param.8) | data formatting | bytes 1882384 | tf_op args[1]
  2.4 26.6 %shard_map.73 = f32[1,1,1024,128]{3,2,1,0:T(8,128)} custom-call(bf16[1,1,1024,128]{3,2,1,0:T(8,128)(2,1)} %res.1, bf16[1,1,4,343,343]{4,3,2,1,0:T(8,128)(2,1)} %copy.8.inner_inv, s32[1,1,4,343]{3,2,1,0:T(4,128)} %inner_idx.1, s32[5,1,512]{2,1,0:T(1,128)} %bitcast.3, bf16[1,1,5,3,343,343]{5,4,3,2,1,0:T(8,128)(2,1)} %face_inv.1, s32[15,1,343]{2,1,0:T(1,128)} %bitcast.2, ...), custom_call_target="tpu_custom_call" | custom-call | tf_op jit(solution)/shard_map/pallas_call | solution.py:234
  29.0 1.9 %copy.10 = f32[1,1,1024,128]{3,2,1,0:T(8,128)} copy(f32[1,1,1024,128]{3,2,1,0:T(8,128)} %shard_map.73) | data formatting | bytes 1048576
where the time goes:
time: 31.1 us; the launch traced here: 30.8 us
  Pallas kernels  26.6 us (86%)
  local copies, waits for them, and re-layouts  4.22 us (14%)
    pallas_call x1, Pallas kernels, on_device(): pl.pallas_call(make_kernel(ndof, nrhs, nint, star, levels, slots, slab, e...  26.6 us
    unnamed x2, local copies, waits for them, and re-layouts  4.22 us

commit v1 on v0

v1 whole, which is shorter than its diff:
```python
import jax
import jax.numpy as jnp
from jax import lax
from jax.experimental import pallas as pl
from jax.experimental.pallas import tpu as pltpu
from jax.sharding import PartitionSpec as P

CUTLV = 3
LANES = 128
CHUNK = 128
INDEX = jnp.int16
STEPS = 32766.0
FLOOR = 1e-30
MESH = pl.DeviceIdType.MESH


def round_up(value, step):
    return (value + step - 1) // step * step


def split_pair(values):
    high = values.astype(jnp.bfloat16)
    low = (values - high.astype(jnp.float32)).astype(jnp.bfloat16)
    return high, low


def make_kernel(ndof, nrhs, nint, star, levels, slots, slab, first, early, late):
    pad = round_up(star, LANES)
    joint = 2 * slab

    def kernel(
        res, inner_inv, inner_idx, dofs, face_inv, face_idx, counts, out,
        inv_in, mixed, inv_face, rows, res_t, st_in, st_face, p_t,
        gathered, gathered_in, pair, pair_in, joined, kept, terms, peaks, back, back_peaks,
        total, acc,
        inv_sem, send_sem, recv_sem, give_sem, back_sem, peak_sem, back_peak_sem,
    ):
        copies = [pltpu.make_async_copy(inner_inv.at[0, 0], inv_in, inv_sem.at[levels])]
        for k in range(levels):
            copies.append(
                pltpu.make_async_copy(face_inv.at[0, 0, k], inv_face.at[k], inv_sem.at[k])
            )
        for copy in copies:
            copy.start()

        places = []
        for k in range(levels):
            axis = "cut" if k < CUTLV else "sub"
            bits = lax.axis_size(axis).bit_length() - 1
            apart = bits - 1 - (k if k < CUTLV else k - CUTLV)
            me = lax.axis_index(axis)
            upper = lax.rem(lax.div(me, 1 << apart), 2)
            far = me + (1 - 2 * upper) * (1 << apart)
            places.append(({axis: far}, upper, 1 - upper))

        barrier = pltpu.get_barrier_semaphore()
        for target, _, _ in places:
            pl.semaphore_signal(barrier, inc=1, device_id=target, device_id_type=MESH)

        def down(row, first, height):
            shape = (height, row.shape[1])
            spots = (lax.broadcasted_iota(jnp.int32, shape, 0) + first).astype(INDEX)
            wanted = jnp.broadcast_to(row, shape).astype(INDEX)
            one, zero = jnp.bfloat16(1), jnp.bfloat16(0)
            return jnp.where(wanted == spots, one, zero)

        def build_slab(k):
            for first in range(0, ndof, CHUNK):
                p_t[first : first + CHUNK, k * slab : (k + 1) * slab] = down(
                    dofs[k], first, CHUNK
                )

        def build_stars(target, row_of, count, height):
            for first in range(0, height, CHUNK):
                for j in range(count):
                    row = rows[row_of + j : row_of + j + 1, :]
                    target[first : first + CHUNK, j * pad : (j + 1) * pad] = down(
                        row, first, CHUNK
                    )

        def build_face(k):
            build_stars(st_face.at[k], nint + k * slots, slots, joint)

        send, give, give_peak = [], [], []
        for k, (target, own, far) in enumerate(places):
            send.append(
                pltpu.make_async_remote_copy(
                    src_ref=joined.at[k, own],
                    dst_ref=joined.at[k, own],
                    send_sem=send_sem.at[k],
                    recv_sem=recv_sem.at[k],
                    device_id=target,
                    device_id_type=MESH,
                )
            )
            give.append(
                pltpu.make_async_remote_copy(
                    src_ref=terms.at[k],
                    dst_ref=back.at[k],
                    send_sem=give_sem.at[k],
                    recv_sem=back_sem.at[k],
                    device_id=target,
                    device_id_type=MESH,
                )
            )
            give_peak.append(
                pltpu.make_async_remote_copy(
                    src_ref=peaks.at[k],
                    dst_ref=back_peaks.at[k],
                    send_sem=peak_sem.at[k],
                    recv_sem=back_peak_sem.at[k],
                    device_id=target,
                    device_id_type=MESH,
                )
            )

        def gather_slab(k):
            build_slab(k)
            own = places[k][1]
            mine = jnp.dot(
                res_t[...], p_t[:, k * slab : (k + 1) * slab], preferred_element_type=jnp.float32
            )
            joined[k, own] = mine.astype(jnp.bfloat16)

        def solve(inverses, picked, pairs, count):
            for j in range(count):
                solved = lax.dot_general(
                    inverses[j],
                    picked[:, j * pad : j * pad + star],
                    (((1,), (1,)), ((), ())),
                    preferred_element_type=jnp.float32,
                )
                high, low = split_pair(solved)
                pairs[j * pad : j * pad + star, 0:nrhs] = high
                pairs[j * pad : j * pad + star, nrhs : 2 * nrhs] = low

        def clear(pairs, count):
            edge = star // 16 * 16
            for j in range(count):
                pairs[j * pad + edge : (j + 1) * pad, :] = jnp.zeros(
                    (pad - edge, 2 * nrhs), jnp.bfloat16
                )

        def front(k):
            picked = jnp.dot(
                joined[k, 0], st_face[k, 0:slab, :], preferred_element_type=jnp.float32
            ) + jnp.dot(
                joined[k, 1], st_face[k, slab:joint, :], preferred_element_type=jnp.float32
            )
            gathered[k] = picked.astype(jnp.bfloat16)
            solve(inv_face.at[k], gathered.at[k], pair.at[k], slots)

        def half_terms(k, half):
            parts = []
            for first in range(0, slab, slab // 2):
                at = pl.multiple_of(half * slab + first, slab // 2)
                both = jnp.dot(
                    st_face[k, pl.ds(at, slab // 2), :],
                    pair[k],
                    preferred_element_type=jnp.float32,
                )
                parts.append(both[:, :nrhs] + both[:, nrhs:])
            return jnp.concatenate(parts, axis=0)

        def far_half(k):
            given = half_terms(k, places[k][2])
            peak = jnp.maximum(jnp.max(jnp.abs(given), axis=0, keepdims=True), FLOOR)
            peaks[k] = jnp.broadcast_to(peak, peaks.shape[1:])
            terms[k] = jnp.round(given * (STEPS / peak)).astype(jnp.int32).astype(jnp.int16)

        def own_half(k):
            kept[k] = half_terms(k, places[k][1])

        def sent(k):
            give_peak[k].start()
            give[k].start()

        def arrived(k):
            send[k].wait_recv()
            copies[1 + k].wait()

        def returned(k):
            give_peak[k].wait_recv()
            give[k].wait_recv()

        def combine(k):
            unit = back_peaks[k, 0:1, :] * (1.0 / STEPS)
            high, low = split_pair(kept[k] + back[k].astype(jnp.int32).astype(jnp.float32) * unit)
            total[k * slab : (k + 1) * slab, 0:nrhs] = high
            total[k * slab : (k + 1) * slab, nrhs : 2 * nrhs] = low

        def spread(target, low, high):
            for first in range(0, ndof, ndof // 2):
                here = slice(first, first + ndof // 2)
                both = jnp.dot(
                    p_t[here, low * slab : high * slab],
                    total[low * slab : high * slab, :],
                    preferred_element_type=jnp.float32,
                )
                target[here, :] = acc[here, :] + (both[:, :nrhs] + both[:, nrhs:])

        def inner_front():
            build_stars(st_in, 0, nint, ndof)
            clear(pair_in, nint)
            picked = jnp.dot(res_t[...], st_in[...], preferred_element_type=jnp.float32)
            gathered_in[...] = picked.astype(jnp.bfloat16)
            copies[0].wait()
            stack = inv_in[...].reshape(star * nint, star)
            lanes = [gathered_in[:, j * pad : j * pad + star] for j in range(nint)]
            turn = lax.broadcasted_iota(jnp.int32, (star * nint, nrhs), 0) % nint
            chosen = None
            for j in range(nint):
                solved = lax.dot_general(
                    stack,
                    lanes[j],
                    (((1,), (1,)), ((), ())),
                    preferred_element_type=jnp.float32,
                )
                chosen = solved if j == 0 else jnp.where(turn == j, solved, chosen)
            mixed[...] = chosen
            for j in range(nint):
                high, low = split_pair(mixed[pl.ds(j, star, stride=nint), :])
                pair_in[j * pad : j * pad + star, 0:nrhs] = high
                pair_in[j * pad : j * pad + star, nrhs : 2 * nrhs] = low

        def inner_back():
            for first in range(0, ndof, ndof // 2):
                here = slice(first, first + ndof // 2)
                both = jnp.dot(st_in[here, :], pair_in[...], preferred_element_type=jnp.float32)
                acc[here, :] = both[:, :nrhs] + both[:, nrhs:]

        def fill_rows():
            rows[...] = jnp.full(rows.shape, -1, jnp.int32)
            rows[0:nint, 0:star] = inner_idx[0, 0]
            for k in range(levels):
                for j in range(slots):
                    at = nint + k * slots + j
                    live = j < counts[0, 0, k]
                    rows[at : at + 1, 0:star] = jnp.where(live, face_idx[k * slots + j], -1)

        res_t[...] = res[0, 0].T
        gather_slab(first)
        pl.semaphore_wait(barrier, levels)
        send[first].start()
        rest = [k for k in range(levels) if k != first]
        for k in rest:
            gather_slab(k)
            send[k].start()

        fill_rows()
        inner_front()
        order = early + late
        build_face(order[0])
        for at, k in enumerate(order):
            arrived(k)
            clear(pair.at[k], slots)
            front(k)
            if at + 1 < len(order):
                build_face(order[at + 1])
            far_half(k)
            sent(k)
        inner_back()
        for k in early:
            own_half(k)
        for k in early:
            returned(k)
            combine(k)
        spread(acc, min(early), max(early) + 1)
        for k in late:
            own_half(k)
        for k in late:
            returned(k)
            combine(k)
            spread(out.at[0, 0] if k == late[-1] else acc, k, k + 1)
        for k in range(levels):
            send[k].wait_send()
            give[k].wait_send()
            give_peak[k].wait_send()

    return kernel


def on_device(
    residual, inner_inverse, inner_index, slab_dofs, face_inverse, face_index, face_count
):
    ndof, nrhs = residual.shape[2:]
    nint, star = inner_index.shape[2:]
    levels, slots = face_index.shape[2:4]
    slab = slab_dofs.shape[3]
    pad = round_up(star, LANES)
    joint = 2 * slab
    index_rows = round_up(nint + levels * slots, 8)
    first, early, late = 0, (4, 3, 2), (0, 1)
    kinds = jnp.bfloat16
    vmem = pl.BlockSpec(memory_space=pltpu.VMEM)
    anywhere = pl.BlockSpec(memory_space=pl.ANY)
    scalar = pl.BlockSpec(memory_space=pltpu.SMEM)
    return pl.pallas_call(
        make_kernel(ndof, nrhs, nint, star, levels, slots, slab, first, early, late),
        out_shape=jax.ShapeDtypeStruct(residual.shape, jnp.float32),
        in_specs=[vmem, anywhere, vmem, vmem, anywhere, vmem, scalar],
        out_specs=vmem,
        scratch_shapes=[
            pltpu.VMEM((star, nint, star), kinds),
            pltpu.VMEM((star * nint, nrhs), jnp.float32),
            pltpu.VMEM((levels, slots, star, star), kinds),
            pltpu.VMEM((index_rows, pad), jnp.int32),
            pltpu.VMEM((nrhs, ndof), kinds),
            pltpu.VMEM((ndof, nint * pad), kinds),
            pltpu.VMEM((levels, joint, slots * pad), kinds),
            pltpu.VMEM((ndof, levels * slab), kinds),
            pltpu.VMEM((levels, nrhs, slots * pad), kinds),
            pltpu.VMEM((nrhs, nint * pad), kinds),
            pltpu.VMEM((levels, slots * pad, 2 * nrhs), kinds),
            pltpu.VMEM((nint * pad, 2 * nrhs), kinds),
            pltpu.VMEM((levels, 2, nrhs, slab), kinds),
            pltpu.VMEM((levels, slab, nrhs), jnp.float32),
            pltpu.VMEM((levels, slab, nrhs), jnp.int16),
            pltpu.VMEM((levels, 8, nrhs), jnp.float32),
            pltpu.VMEM((levels, slab, nrhs), jnp.int16),
            pltpu.VMEM((levels, 8, nrhs), jnp.float32),
            pltpu.VMEM((levels * slab, 2 * nrhs), kinds),
            pltpu.VMEM((ndof, nrhs), jnp.float32),
            pltpu.SemaphoreType.DMA((levels + 1,)),
            pltpu.SemaphoreType.DMA((levels,)),
            pltpu.SemaphoreType.DMA((levels,)),
            pltpu.SemaphoreType.DMA((levels,)),
            pltpu.SemaphoreType.DMA((levels,)),
            pltpu.SemaphoreType.DMA((levels,)),
            pltpu.SemaphoreType.DMA((levels,)),
        ],
        compiler_params=pltpu.CompilerParams(
            collective_id=0, has_side_effects=True, vmem_limit_bytes=55300000
        ),
    )(
        *(
            pltpu.with_memory_space_constraint(value, pltpu.HBM)
            for value in (
        residual,
        jnp.swapaxes(inner_inverse, 2, 3),
        inner_index,
        slab_dofs.reshape(levels, 1, slab),
        face_inverse,
        face_index.reshape(levels * slots, 1, star),
        face_count,
            )
        )
    )


def solution(mesh):
    return jax.shard_map(
        on_device,
        mesh=mesh,
        in_specs=(
            P("cut", "sub", None, None),
            P("cut", "sub", None, None, None),
            P("cut", "sub", None, None),
            P("cut", "sub", None, None),
            P("cut", "sub", None, None, None, None),
            P("cut", "sub", None, None, None),
            P("cut", "sub", None),
        ),
        out_specs=P("cut", "sub", None, None),
        check_vma=False,
    )
```

time: 31.1 us -> 24.3 us (0.78)
  local copies, waits for them, and re-layouts: 4.22 us -> 0.8 us
  Pallas kernels: 26.6 us -> 23.4 us
    unnamed x2 -> x1, local copies, waits for them, and re-layouts: 4.22 us -> 0.8 us
    pallas_call x1, Pallas kernels: 26.6 us -> 23.4 us  [on_device(): pl.pallas_call(make_kernel(ndof, nrhs, nint, star, levels, slots, slab, f...]
where the time goes in v1:
time: 24.3 us; the launch traced here: 24.2 us
  Pallas kernels  23.4 us (96%)
  local copies, waits for them, and re-layouts  0.8 us (3%)
    pallas_call x1, Pallas kernels, on_device(): pl.pallas_call(make_kernel(ndof, nrhs, nint, star, levels, slots, slab, f...  23.4 us
    unnamed x1, local copies, waits for them, and re-layouts  0.8 us

profile of v1, /device:TPU:0, one launch (start us, length us, event | category | flops | bytes accessed | tf_op | source)
XLA Modules:
  0.0 24.2 jit_solution(2737965234540473081)
XLA Ops:
  0.0 23.4 %shard_map.73 = f32[1,1,1024,128]{3,2,1,0:T(8,128)S(1)} custom-call(bf16[1,1,1024,128]{3,2,1,0:T(8,128)(2,1)} %res.1, bf16[1,1,343,4,343]{4,3,2,1,0:T(4,128)(2,1)} %bitcast.3, s32[1,1,4,343]{3,2,1,0:T(4,128)} %inner_idx.1, s32[5,1,512]{2,1,0:T(1,128)} %bitcast.5, bf16[1,1,5,3,343,343]{5,4,3,2,1,0:T(8,128)(2,1)} %face_inv.1, s32[15,1,343]{2,1,0:T(1,128)} %bitcast.4, ...), custom_call_target="tpu_custom_call" | custom-call | tf_op jit(solution)/shard_map/pallas_call | solution.py:298
  23.4 0.8 %copy.9 = f32[1,1,1024,128]{3,2,1,0:T(8,128)} copy(f32[1,1,1024,128]{3,2,1,0:T(8,128)S(1)} %shard_map.73) | data formatting | bytes 1048576

commit v2 on v1

--- a/solution.py
+++ b/solution.py
@@ -27,6 +27,8 @@
 def make_kernel(ndof, nrhs, nint, star, levels, slots, slab, first, early, late):
     pad = round_up(star, LANES)
     joint = 2 * slab
+
+    building = ((1,), (2, 3), (4,), (), ())
 
     def kernel(
         res, inner_inv, inner_idx, dofs, face_inv, face_idx, counts, out,
@@ -40,8 +42,7 @@
             copies.append(
                 pltpu.make_async_copy(face_inv.at[0, 0, k], inv_face.at[k], inv_sem.at[k])
             )
-        for copy in copies:
-            copy.start()
+        copies[0].start()
 
         places = []
         for k in range(levels):
@@ -242,21 +243,31 @@
         gather_slab(first)
         pl.semaphore_wait(barrier, levels)
         send[first].start()
-        rest = [k for k in range(levels) if k != first]
+        for k in (4, 3, 2, 0, 1):
+            copies[1 + k].start()
+        rest = range(first + 1, levels)
         for k in rest:
-            gather_slab(k)
+            build_slab(k)
+        from_rest = (first + 1) * slab
+        mine = jnp.dot(
+            res_t[...], p_t[:, from_rest : levels * slab], preferred_element_type=jnp.float32
+        )
+        for k in rest:
+            at = k * slab - from_rest
+            joined[k, places[k][1]] = mine[:, at : at + slab].astype(jnp.bfloat16)
+        for k in rest:
             send[k].start()
 
         fill_rows()
         inner_front()
-        order = early + late
+        order = (4, 3, 0, 2, 1)
         build_face(order[0])
         for at, k in enumerate(order):
             arrived(k)
             clear(pair.at[k], slots)
             front(k)
-            if at + 1 < len(order):
-                build_face(order[at + 1])
+            for ahead in building[at]:
+                build_face(order[ahead])
             far_half(k)
             sent(k)
         inner_back()
@@ -330,7 +341,7 @@
             pltpu.SemaphoreType.DMA((levels,)),
         ],
         compiler_params=pltpu.CompilerParams(
-            collective_id=0, has_side_effects=True, vmem_limit_bytes=55300000
+            collective_id=0, has_side_effects=True, vmem_limit_bytes=50000000
         ),
     )(
         *(

time: 24.3 us -> 23.8 us (0.979)
  Pallas kernels: 23.4 us -> 22.9 us
    pallas_call x1, Pallas kernels: 23.4 us -> 22.9 us  [on_device(): pl.pallas_call(make_kernel(ndof, nrhs, nint, star, levels, slots, slab, f...]
where the time goes in v2:
time: 23.8 us; the launch traced here: 23.7 us
  Pallas kernels  22.9 us (96%)
  local copies, waits for them, and re-layouts  0.8 us (3%)
    pallas_call x1, Pallas kernels, on_device(): pl.pallas_call(make_kernel(ndof, nrhs, nint, star, levels, slots, slab, f...  22.9 us
    unnamed x1, local copies, waits for them, and re-layouts  0.8 us

profile of v2, /device:TPU:0, one launch (start us, length us, event | category | flops | bytes accessed | tf_op | source)
XLA Modules:
  0.0 23.7 jit_solution(14584834199311097332)
XLA Ops:
  0.0 22.9 %shard_map.73 = f32[1,1,1024,128]{3,2,1,0:T(8,128)S(1)} custom-call(bf16[1,1,1024,128]{3,2,1,0:T(8,128)(2,1)} %res.1, bf16[1,1,343,4,343]{4,3,2,1,0:T(4,128)(2,1)} %bitcast.3, s32[1,1,4,343]{3,2,1,0:T(4,128)} %inner_idx.1, s32[5,1,512]{2,1,0:T(1,128)} %bitcast.5, bf16[1,1,5,3,343,343]{5,4,3,2,1,0:T(8,128)(2,1)} %face_inv.1, s32[15,1,343]{2,1,0:T(1,128)} %bitcast.4, ...), custom_call_target="tpu_custom_call" | custom-call | tf_op jit(solution)/shard_map/pallas_call | solution.py:309
  22.9 0.8 %copy.9 = f32[1,1,1024,128]{3,2,1,0:T(8,128)} copy(f32[1,1,1024,128]{3,2,1,0:T(8,128)S(1)} %shard_map.73) | data formatting | bytes 1048576
